TPU v7x, 32 devices: a whole 2x2x4 slice. The times are simulated.
32 devices in a mesh: groups: 2 (over y), rows: 4 (over z), cols: 4 (over x, core).
Axes of the slice: x: 2, y: 2, z: 4, core: 2. Of those that a mesh axis runs over, the one named last changes fastest.
Arguments:
- tile_blocks: float32 [32, 32, 4, 128, 128], P(('groups', 'rows'), 'cols'), parts along dimension 0, may hold values from -1 to 3
- tile_codes: int32 [32, 32, 3], P(('groups', 'rows'), 'cols'), parts along dimension 0, may hold values from 0 to 3, as said below
- shifts: float32 [16], P('groups'), parts along dimension 0, may hold values from 1.2 to 2.8
- shift_order: int32 [16], P('groups'), parts along dimension 0, may hold values from 0 to 7, each once
- earlier: float32 [16, 32, 32, 128], P(None, ('groups', 'rows'), 'cols'), parts along dimension 1, may hold values from -60 to 60
- start_weights: float32 [32], P('groups'), parts along dimension 0, may hold values from -1 to 1
Outputs:
- new_basis: float32 [8, 32, 32, 128], P(None, ('groups', 'rows'), 'cols'), parts along dimension 1
- upper_factor: float32 [16, 8], P('groups'), parts along dimension 0
- projections: float32 [32, 8], P('groups'), parts along dimension 0
There are 2 independent parts, one for each index of `groups`. A program takes and returns all parts, laid end to end along the dimension named above; each array names one. Nothing has to cross between parts.
Inputs may be any that keep to these rules, and one draw needn't show every extreme that they name: `tile_codes`: the three codes of one block are distinct. `shift_order`: each of 0 to 7 appears once.
All inputs are finite; a program needn't handle non-finite values.
Results may differ from a plain program's by a relative error of at most 0.0003.
Values sent between devices are 32-bit elements; how exact they have to be, the bound alone decides.
A program may use at most 64 MiB of HBM per device.

v0:
```python
import functools

import jax
import jax.numpy as jnp
from jax import lax
from jax.experimental import pallas as pl
from jax.experimental.pallas import tpu as pltpu
from jax.sharding import PartitionSpec as P

MESH = pl.DeviceIdType.MESH
ABOVE, BELOW, LEFT, RIGHT = range(4)


def kernel(
    n_rows, n_cols,
    blocks_hbm, codes_ref, shifts_ref, order_ref, earlier_hbm, weights_ref,
    basis_ref, upper_ref, proj_ref,
    blocks, earlier, fields, chosen, halo_rows, halo_cols, edge_cols, stats, gathered, spread,
    load_sem, earlier_sem, send_sem, recv_sem, all_send, all_recv,
):
    rows, cols, slots, tile, _ = blocks.shape
    basis = basis_ref.shape[0]
    prev = earlier.shape[0]
    groups_prev = prev // basis
    peers = n_rows * n_cols
    cells = float(peers * rows * cols * tile)
    my_row, my_col = lax.axis_index("rows"), lax.axis_index("cols")
    me = my_row * n_cols + my_col

    def load(r, c):
        return pltpu.make_async_copy(
            blocks_hbm.at[r, c], blocks.at[r, c], load_sem.at[r, c]
        )

    earlier_copy = pltpu.make_async_copy(earlier_hbm, earlier, earlier_sem)
    earlier_copy.start()
    rim_rows = [0, rows - 1]
    middle = list(range(1, rows - 1))
    for r in rim_rows:
        for c in range(cols):
            load(r, c).start()
    for r in middle:
        for c in (0, cols - 1):
            load(r, c).start()
    for r in middle:
        for c in range(1, cols - 1):
            load(r, c).start()

    barrier = pltpu.get_barrier_semaphore()

    def place(index):
        return {"rows": index // n_cols, "cols": index % n_cols}

    @pl.loop(1, peers)
    def _(d):
        pl.semaphore_signal(
            barrier, inc=1, device_id=place((me + d) % peers), device_id_type=MESH
        )

    for k in range(1, basis + 1):
        fields[k] = jnp.zeros((rows, cols, tile), jnp.float32)
    stats[...] = jnp.zeros_like(stats)
    no_row = jnp.zeros((basis, cols, tile), jnp.float32)
    no_col = jnp.zeros((basis, rows, tile), jnp.float32)
    has = [my_row > 0, my_row < n_rows - 1, my_col > 0, my_col < n_cols - 1]

    @pl.when(my_row == 0)
    def _():
        halo_rows[:, 0] = no_row

    @pl.when(my_row == n_rows - 1)
    def _():
        halo_rows[:, 1] = no_row

    @pl.when(my_col == 0)
    def _():
        halo_cols[:, 0] = no_col

    @pl.when(my_col == n_cols - 1)
    def _():
        halo_cols[:, 1] = no_col

    def hop(k, direction):
        if direction == ABOVE:
            src, dst, where_to = fields.at[k, 0], halo_rows.at[k, 1], {"rows": my_row - 1}
        elif direction == BELOW:
            src, dst, where_to = fields.at[k, rows - 1], halo_rows.at[k, 0], {"rows": my_row + 1}
        elif direction == LEFT:
            src, dst, where_to = edge_cols.at[k, 0], halo_cols.at[k, 1], {"cols": my_col - 1}
        else:
            src, dst, where_to = edge_cols.at[k, 1], halo_cols.at[k, 0], {"cols": my_col + 1}
        return pltpu.make_async_remote_copy(
            src_ref=src,
            dst_ref=dst,
            send_sem=send_sem.at[k, direction],
            recv_sem=recv_sem.at[k, direction ^ 1],
            device_id=where_to,
            device_id_type=MESH,
        )

    def arrival(k, direction):
        if direction in (ABOVE, BELOW):
            dst = halo_rows.at[k, direction]
        else:
            dst = halo_cols.at[k, direction - 2]
        return pltpu.make_async_copy(dst, dst, recv_sem.at[k, direction])

    def send(k, directions):
        for direction in directions:
            @pl.when(has[direction])
            def _(direction=direction):
                hop(k, direction).start()

    def receive(k):
        for direction in range(4):
            @pl.when(has[direction])
            def _(direction=direction):
                arrival(k, direction).wait()

    codes = codes_ref[...]
    masks = [
        [
            jnp.broadcast_to(codes[r, :, s : s + 1], (cols, tile))
            for r in range(rows)
        ]
        for s in range(slots - 1)
    ]
    sublane = lax.broadcasted_iota(jnp.int32, (cols, tile), 0)
    lane = lax.broadcasted_iota(jnp.int32, (basis, tile), 1)

    def choose(k):
        for r in range(rows):
            here = fields[k, r]
            above = fields[k, r - 1] if r > 0 else halo_rows[k, 0]
            below = fields[k, r + 1] if r < rows - 1 else halo_rows[k, 1]
            left = jnp.where(sublane == 0, halo_cols[k, 0, r : r + 1], pltpu.roll(here, 1, 0))
            right = jnp.where(
                sublane == cols - 1, halo_cols[k, 1, r : r + 1], pltpu.roll(here, cols - 1, 0)
            )
            chosen[0, r] = here
            for s in range(slots - 1):
                code = masks[s][r]
                chosen[s + 1, r] = jnp.where(
                    code < 2,
                    jnp.where(code == 0, above, below),
                    jnp.where(code == 2, left, right),
                )

    def cell(k, shift, r, c):
        total = blocks[r, c, 0] * chosen[0, r, c : c + 1]
        for s in range(1, slots):
            total = total + blocks[r, c, s] * chosen[s, r, c : c + 1]
        product = jnp.sum(total.T, axis=0, keepdims=True)
        fields[k + 1, r, c : c + 1] = product - shift * chosen[0, r, c : c + 1]

    def row_of_cells(k, shift, r, columns, first):
        for c in columns:
            if first:
                load(r, c).wait()
            cell(k, shift, r, c)

    def inner(k):
        field = fields[k + 1]
        merged = stats[...]
        for g in range(groups_prev + 1):
            if g < groups_prev:
                other = earlier[g * basis : (g + 1) * basis]
            else:
                other = fields[1 : basis + 1]
            pair = jnp.sum(jnp.sum(other * field[None], axis=1), axis=1)
            value = jnp.sum(pair, axis=1, keepdims=True)
            merged = jnp.where(lane == g * basis + k, value, merged)
        stats[...] = merged

    def step(k, first):
        shift = shifts_ref[order_ref[k]]
        receive(k)
        choose(k)

        @pl.loop(0, 2)
        def _(side):
            row_of_cells(k, shift, side * (rows - 1), range(cols), first)

        last = isinstance(k, int) and k == basis - 1
        if not last:
            send(k + 1, (ABOVE, BELOW))

        @pl.loop(1, rows - 1)
        def _(r):
            row_of_cells(k, shift, r, (0, cols - 1), first)

        if not last:
            for r in range(rows):
                edge_cols[k + 1, 0, r : r + 1] = fields[k + 1, r, 0:1]
                edge_cols[k + 1, 1, r : r + 1] = fields[k + 1, r, cols - 1 : cols]
            send(k + 1, (LEFT, RIGHT))

        @pl.loop(1, rows - 1)
        def _(r):
            row_of_cells(k, shift, r, range(1, cols - 1), first)

        inner(k)

    earlier_copy.wait()
    start = weights_ref[0] * earlier[0]
    for p in range(1, prev):
        start = start + weights_ref[p] * earlier[p]
    fields[0] = start
    for r in range(rows):
        edge_cols[0, 0, r : r + 1] = fields[0, r, 0:1]
        edge_cols[0, 1, r : r + 1] = fields[0, r, cols - 1 : cols]
    pl.semaphore_wait(barrier, peers - 1)
    send(0, (ABOVE, BELOW, LEFT, RIGHT))
    step(0, True)

    @pl.loop(1, basis - 1)
    def _(k):
        step(k, False)

    step(basis - 1, False)

    def deliver(d):
        return pltpu.make_async_remote_copy(
            src_ref=stats,
            dst_ref=gathered.at[me],
            send_sem=all_send.at[d],
            recv_sem=all_recv.at[me],
            device_id=place((me + d) % peers),
            device_id_type=MESH,
        )

    @pl.loop(1, peers)
    def _(d):
        deliver(d).start()

    gathered[me] = stats[...]

    @pl.loop(1, peers)
    def _(d):
        source = (me + d) % peers
        pltpu.make_async_copy(
            gathered.at[source], gathered.at[source], all_recv.at[source]
        ).wait()

    total = jnp.sum(gathered[...], axis=0) * (1.0 / cells)
    proj = []
    for i in range((groups_prev + 1) * basis):
        column = jnp.broadcast_to(total[:, i : i + 1], (basis, tile))
        spread[i] = column
        proj.append(column)
    for g in range(groups_prev):
        proj_ref[g * basis : (g + 1) * basis, :] = total[:, g * basis : (g + 1) * basis]

    cleaned = []
    for k in range(basis):
        value = fields[k + 1]
        for p in range(prev):
            g, q = p // basis, p % basis
            value = value - spread[g * basis + k, q : q + 1][None] * earlier[p]
        basis_ref[k] = value

    gram = {}
    for j in range(basis):
        for k in range(j, basis):
            removed = proj[j] * proj[k]
            for g in range(1, groups_prev):
                removed = removed + proj[g * basis + j] * proj[g * basis + k]
            gram[j, k] = spread[groups_prev * basis + k, j : j + 1] - jnp.sum(
                removed, axis=0, keepdims=True
            )
    lower, inverse = {}, []
    for j in range(basis):
        root = jnp.sqrt(gram[j, j])
        inverse.append(1.0 / root)
        lower[j, j] = root
        for k in range(j + 1, basis):
            lower[k, j] = gram[j, k] * inverse[j]
        for k in range(j + 1, basis):
            for m in range(k, basis):
                gram[k, m] = gram[k, m] - lower[k, j] * lower[m, j]

    row_index = lax.broadcasted_iota(jnp.int32, (basis, tile), 0)
    upper = jnp.zeros((basis, tile), jnp.float32)
    for j in range(basis):
        line = jnp.zeros((1, tile), jnp.float32)
        for k in range(j, basis):
            line = jnp.where(lane[0:1] == k, lower[k, j], line)
        upper = jnp.where(row_index == j, line, upper)
    upper_ref[...] = upper[:, :basis]

    for r in range(rows):
        done = []
        for k in range(basis):
            value = basis_ref[k, r]
            for j in range(k):
                value = value - lower[k, j] * done[j]
            value = value * inverse[k]
            done.append(value)
            basis_ref[k, r] = value

    @pl.loop(0, basis)
    def _(k):
        for direction in range(4):
            @pl.when(has[direction])
            def _(direction=direction):
                hop(k, direction).wait_send()

    @pl.loop(1, peers)
    def _(d):
        deliver(d).wait_send()


def shards(n_rows, n_cols, tile_blocks, tile_codes, shifts, shift_order, earlier, start_weights):
    rows, cols, slots, tile, _ = tile_blocks.shape
    basis, prev = shifts.shape[0], earlier.shape[0]
    peers = n_rows * n_cols
    vmem = pl.BlockSpec(memory_space=pltpu.VMEM)
    smem = pl.BlockSpec(memory_space=pltpu.SMEM)
    anywhere = pl.BlockSpec(memory_space=pl.ANY)
    f32 = jnp.float32
    return pl.pallas_call(
        functools.partial(kernel, n_rows, n_cols),
        out_shape=(
            jax.ShapeDtypeStruct((basis, rows, cols, tile), f32),
            jax.ShapeDtypeStruct((basis, basis), f32),
            jax.ShapeDtypeStruct((prev, basis), f32),
        ),
        in_specs=[anywhere, vmem, smem, smem, anywhere, smem],
        out_specs=(vmem, vmem, vmem),
        scratch_shapes=[
            pltpu.VMEM(tile_blocks.shape, f32),
            pltpu.VMEM(earlier.shape, f32),
            pltpu.VMEM((basis + 1, rows, cols, tile), f32),
            pltpu.VMEM((slots, rows, cols, tile), f32),
            pltpu.VMEM((basis, 2, cols, tile), f32),
            pltpu.VMEM((basis, 2, rows, tile), f32),
            pltpu.VMEM((basis, 2, rows, tile), f32),
            pltpu.VMEM((basis, tile), f32),
            pltpu.VMEM((peers, basis, tile), f32),
            pltpu.VMEM(((prev // basis + 1) * basis, basis, tile), f32),
            pltpu.SemaphoreType.DMA((rows, cols)),
            pltpu.SemaphoreType.DMA,
            pltpu.SemaphoreType.DMA((basis, 4)),
            pltpu.SemaphoreType.DMA((basis, 4)),
            pltpu.SemaphoreType.DMA((peers,)),
            pltpu.SemaphoreType.DMA((peers,)),
        ],
        compiler_params=pltpu.CompilerParams(
            collective_id=0, has_side_effects=True, vmem_limit_bytes=48 * 1024 * 1024
        ),
        name="sstep",
    )(tile_blocks, tile_codes, shifts, shift_order, earlier, start_weights)


def solution(mesh):
    in_specs = (
        P(("groups", "rows"), "cols", None, None, None),
        P(("groups", "rows"), "cols", None),
        P("groups"),
        P("groups"),
        P(None, ("groups", "rows"), "cols", None),
        P("groups"),
    )
    out_specs = (P(None, ("groups", "rows"), "cols", None), P("groups", None), P("groups", None))
    body = functools.partial(shards, mesh.shape["rows"], mesh.shape["cols"])
    return jax.shard_map(body, mesh=mesh, in_specs=in_specs, out_specs=out_specs, check_vma=False)
```

profile of v0, /device:TPU:0, one launch (start us, length us, event | category | flops | bytes accessed | tf_op | source)
XLA Modules:
  0.0 44.7 jit_solution(8807182570764063236)
XLA Ops:
  0.6 0.8 %copy.9.codes_ref = s32[4,8,3]{2,1,0:T(8,128)S(1)} copy(s32[4,8,3]{1,0,2:T(4,128)} %param.7) | data formatting | bytes 768 | tf_op args[1]
  1.4 0.0 copy-start
  1.4 0.9 %copy-done = f32[16,4,8,128]{3,2,1,0:T(8,128)S(1)} copy-done((f32[16,4,8,128]{3,2,1,0:T(8,128)S(1)}, f32[16,4,8,128]{3,2,1,0:T(8,128)}, u32[]{:S(2)}) %copy-start) | copy-done | bytes 262168
  2.4 0.0 copy-start.1
  2.4 0.7 %copy-done.1 = f32[8]{0:T(128)S(1)} copy-done((f32[8]{0:T(128)S(1)}, f32[8]{0:T(128)}, u32[]{:S(2)}) %copy-start.1) | copy-done | bytes 56
  3.0 0.0 copy-start.2
  3.0 0.7 %copy-done.2 = s32[8]{0:T(128)S(1)} copy-done((s32[8]{0:T(128)S(1)}, s32[8]{0:T(128)}, u32[]{:S(2)}) %copy-start.2) | copy-done | bytes 56
  3.7 0.0 copy-start.3
  3.7 0.7 %copy-done.3 = f32[16]{0:T(128)S(1)} copy-done((f32[16]{0:T(128)S(1)}, f32[16]{0:T(128)}, u32[]{:S(2)}) %copy-start.3) | copy-done | bytes 88
  4.3 38.4 %sstep.1 = (f32[8,4,8,128]{3,2,1,0:T(8,128)S(1)}, f32[8,8]{1,0:T(8,128)S(1)}, f32[16,8]{1,0:T(8,128)S(1)}) custom-call(f32[4,8,4,128,128]{4,3,2,1,0:T(8,128)} %blocks_hbm.1, s32[4,8,3]{2,1,0:T(8,128)S(1)} %copy.9.codes_ref, f32[8]{0:T(128)S(1)} %copy-done.1, s32[8]{0:T(128)S(1)} %copy-done.2, f32[16,4,8,128]{3,2,1,0:T(8,128)S(1)} %copy-done, f32[16]{0:T(128)S(1)} %copy-done.3), custom_call_target="tpu_custom_call" | custom-call | tf_op jit(solution)/shard_map/sstep/pallas_call | solution.py:321
  42.8 0.7 %copy.10 = f32[16,8]{0,1:T(8,128)} copy(f32[16,8]{1,0:T(8,128)S(1)} %get-tuple-element.5) | data formatting | bytes 1024 | tf_op jit(solution)/shard_map/sstep/pallas_call | solution.py:321
  43.5 0.7 %copy.13 = f32[8,4,8,128]{3,2,1,0:T(8,128)} copy(f32[8,4,8,128]{3,2,1,0:T(8,128)S(1)} %get-tuple-element.9) | data formatting | bytes 262144
  44.1 0.6 %copy.14 = f32[8,8]{1,0:T(8,128)} copy(f32[8,8]{1,0:T(8,128)S(1)} %get-tuple-element.10) | data formatting | bytes 512
Async XLA Ops:
  1.4 0.9 %copy-start = (f32[16,4,8,128]{3,2,1,0:T(8,128)S(1)}, f32[16,4,8,128]{3,2,1,0:T(8,128)}, u32[]{:S(2)}) copy-start(f32[16,4,8,128]{3,2,1,0:T(8,128)} %earlier_hbm.1) | copy-start | bytes 786436
  2.4 0.7 %copy-start.1 = (f32[8]{0:T(128)S(1)}, f32[8]{0:T(128)}, u32[]{:S(2)}) copy-start(f32[8]{0:T(128)} %shifts_ref.1) | copy-start | bytes 100
  3.0 0.7 %copy-start.2 = (s32[8]{0:T(128)S(1)}, s32[8]{0:T(128)}, u32[]{:S(2)}) copy-start(s32[8]{0:T(128)} %order_ref.1) | copy-start | bytes 100
  3.7 0.7 %copy-start.3 = (f32[16]{0:T(128)S(1)}, f32[16]{0:T(128)}, u32[]{:S(2)}) copy-start(f32[16]{0:T(128)} %weights_ref.1) | copy-start | bytes 196
where the time goes:
time: 44.9 us; the launch traced here: 44.7 us
  Pallas kernels  38.4 us (86%)
  local copies, waits for them, and re-layouts  5.61 us (12%)
  between operations  0.64 us (1%)
    pallas_call x1, Pallas kernels, shards(): pl.pallas_call(functools.partial(kernel, n_rows, n_cols), out_shape=(jax....  38.4 us
    unnamed x11, local copies, waits for them, and re-layouts  4.94 us

commit v1 on v0

--- a/solution.py
+++ b/solution.py
@@ -13,10 +13,12 @@
 
 def kernel(
     n_rows, n_cols,
-    blocks_hbm, codes_ref, shifts_ref, order_ref, earlier_hbm, weights_ref,
+    blocks_hbm, codes_hbm, shifts_hbm, order_hbm, earlier_hbm, weights_hbm,
     basis_ref, upper_ref, proj_ref,
-    blocks, earlier, fields, chosen, halo_rows, halo_cols, edge_cols, stats, gathered, spread,
-    load_sem, earlier_sem, send_sem, recv_sem, all_send, all_recv,
+    blocks, earlier, codes_ref, shifts_ref, order_ref, weights_ref,
+    fields, chosen, halo_rows, halo_cols, edge_cols, rim_rows, rim_cols,
+    code_table, stats, gathered, spread,
+    load_sem, small_sem, send_sem, recv_sem, all_send, all_recv,
 ):
     rows, cols, slots, tile, _ = blocks.shape
     basis = basis_ref.shape[0]
@@ -32,18 +34,22 @@
             blocks_hbm.at[r, c], blocks.at[r, c], load_sem.at[r, c]
         )
 
-    earlier_copy = pltpu.make_async_copy(earlier_hbm, earlier, earlier_sem)
-    earlier_copy.start()
-    rim_rows = [0, rows - 1]
-    middle = list(range(1, rows - 1))
-    for r in rim_rows:
+    small = [
+        pltpu.make_async_copy(src, dst, small_sem.at[i])
+        for i, (src, dst) in enumerate(
+            [
+                (weights_hbm, weights_ref),
+                (earlier_hbm, earlier),
+                (codes_hbm, codes_ref),
+                (shifts_hbm, shifts_ref),
+                (order_hbm, order_ref),
+            ]
+        )
+    ]
+    for copy in small:
+        copy.start()
+    for r in range(rows):
         for c in range(cols):
-            load(r, c).start()
-    for r in middle:
-        for c in (0, cols - 1):
-            load(r, c).start()
-    for r in middle:
-        for c in range(1, cols - 1):
             load(r, c).start()
 
     barrier = pltpu.get_barrier_semaphore()
@@ -117,47 +123,96 @@
             def _(direction=direction):
                 arrival(k, direction).wait()
 
-    codes = codes_ref[...]
-    masks = [
-        [
-            jnp.broadcast_to(codes[r, :, s : s + 1], (cols, tile))
-            for r in range(rows)
-        ]
-        for s in range(slots - 1)
-    ]
     sublane = lax.broadcasted_iota(jnp.int32, (cols, tile), 0)
     lane = lax.broadcasted_iota(jnp.int32, (basis, tile), 1)
+    diagonal = lax.broadcasted_iota(jnp.int32, (cols, cols), 0) == lax.broadcasted_iota(
+        jnp.int32, (cols, cols), 1
+    )
+
+    def code_columns():
+        codes = codes_ref[...].astype(jnp.float32)
+        masks = []
+        for s in range(slots - 1):
+            masks.append([])
+            for r in range(rows):
+                line = jnp.broadcast_to(codes[s, r : r + 1], (cols, cols))
+                column = jnp.sum(jnp.where(diagonal, line, 0.0), axis=1, keepdims=True)
+                masks[s].append(jnp.broadcast_to(column, (cols, tile)))
+        return masks
 
     def choose(k):
+        none = jnp.zeros((cols, tile), jnp.float32)
         for r in range(rows):
             here = fields[k, r]
-            above = fields[k, r - 1] if r > 0 else halo_rows[k, 0]
-            below = fields[k, r + 1] if r < rows - 1 else halo_rows[k, 1]
-            left = jnp.where(sublane == 0, halo_cols[k, 0, r : r + 1], pltpu.roll(here, 1, 0))
-            right = jnp.where(
-                sublane == cols - 1, halo_cols[k, 1, r : r + 1], pltpu.roll(here, cols - 1, 0)
-            )
+            above = fields[k, r - 1] if r > 0 else none
+            below = fields[k, r + 1] if r < rows - 1 else none
+            left = jnp.where(sublane == 0, 0.0, pltpu.roll(here, 1, 0))
+            right = jnp.where(sublane == cols - 1, 0.0, pltpu.roll(here, cols - 1, 0))
             chosen[0, r] = here
             for s in range(slots - 1):
-                code = masks[s][r]
+                code = code_table[s, r]
                 chosen[s + 1, r] = jnp.where(
-                    code < 2,
-                    jnp.where(code == 0, above, below),
-                    jnp.where(code == 2, left, right),
+                    code < 1.5,
+                    jnp.where(code < 0.5, above, below),
+                    jnp.where(code < 2.5, left, right),
                 )
 
-    def cell(k, shift, r, c):
-        total = blocks[r, c, 0] * chosen[0, r, c : c + 1]
-        for s in range(1, slots):
-            total = total + blocks[r, c, s] * chosen[s, r, c : c + 1]
-        product = jnp.sum(total.T, axis=0, keepdims=True)
-        fields[k + 1, r, c : c + 1] = product - shift * chosen[0, r, c : c + 1]
-
-    def row_of_cells(k, shift, r, columns, first):
-        for c in columns:
+    def inside(k, first):
+        shift = shifts_ref[order_ref[k]]
+        choose(k)
+
+        @pl.loop(0, rows)
+        def _(r):
             if first:
-                load(r, c).wait()
-            cell(k, shift, r, c)
+                for c in range(cols):
+                    load(r, c).wait()
+            for c in range(cols):
+                total = blocks[r, c, 0] * chosen[0, r, c : c + 1]
+                for s in range(1, slots):
+                    total = total + blocks[r, c, s] * chosen[s, r, c : c + 1]
+                product = jnp.sum(total.T, axis=0, keepdims=True)
+                fields[k + 1, r, c : c + 1] = product - shift * chosen[0, r, c : c + 1]
+
+    def pick(r, c, direction):
+        total = jnp.zeros((tile, tile), jnp.float32)
+        for s in range(slots - 1):
+            code = code_table[s, r, c : c + 1]
+            total = jnp.where(code == float(direction), blocks[r, c, s + 1], total)
+        return total
+
+    def gather_rim():
+        for side in range(2):
+            @pl.loop(0, cols)
+            def _(c, side=side):
+                total = jnp.zeros((tile, tile), jnp.float32)
+                for s in range(slots - 1):
+                    code = code_table[s, side * (rows - 1), pl.ds(c, 1)]
+                    total = jnp.where(
+                        code == float(side), blocks[side * (rows - 1), c, s + 1], total
+                    )
+                rim_rows[side, c] = total
+
+            @pl.loop(0, rows)
+            def _(r, side=side):
+                rim_cols[side, r] = pick(r, side * (cols - 1), side + LEFT)
+
+    def rim(k):
+        for r in range(rows):
+            for c in range(cols):
+                parts = []
+                for side in range(2):
+                    if r == side * (rows - 1):
+                        parts.append(rim_rows[side, c] * halo_rows[k, side, c : c + 1])
+                    if c == side * (cols - 1):
+                        parts.append(rim_cols[side, r] * halo_cols[k, side, r : r + 1])
+                if parts:
+                    product = jnp.sum(sum(parts[1:], parts[0]).T, axis=0, keepdims=True)
+                    fields[k + 1, r, c : c + 1] += product
+
+    def edges(k):
+        for r in range(rows):
+            edge_cols[k, 0, r : r + 1] = fields[k, r, 0:1]
+            edge_cols[k, 1, r : r + 1] = fields[k, r, cols - 1 : cols]
 
     def inner(k):
         field = fields[k + 1]
@@ -172,52 +227,35 @@
             merged = jnp.where(lane == g * basis + k, value, merged)
         stats[...] = merged
 
-    def step(k, first):
-        shift = shifts_ref[order_ref[k]]
-        receive(k)
-        choose(k)
-
-        @pl.loop(0, 2)
-        def _(side):
-            row_of_cells(k, shift, side * (rows - 1), range(cols), first)
-
-        last = isinstance(k, int) and k == basis - 1
-        if not last:
-            send(k + 1, (ABOVE, BELOW))
-
-        @pl.loop(1, rows - 1)
-        def _(r):
-            row_of_cells(k, shift, r, (0, cols - 1), first)
-
-        if not last:
-            for r in range(rows):
-                edge_cols[k + 1, 0, r : r + 1] = fields[k + 1, r, 0:1]
-                edge_cols[k + 1, 1, r : r + 1] = fields[k + 1, r, cols - 1 : cols]
-            send(k + 1, (LEFT, RIGHT))
-
-        @pl.loop(1, rows - 1)
-        def _(r):
-            row_of_cells(k, shift, r, range(1, cols - 1), first)
-
-        inner(k)
-
-    earlier_copy.wait()
+    small[0].wait()
+    small[1].wait()
     start = weights_ref[0] * earlier[0]
     for p in range(1, prev):
         start = start + weights_ref[p] * earlier[p]
     fields[0] = start
-    for r in range(rows):
-        edge_cols[0, 0, r : r + 1] = fields[0, r, 0:1]
-        edge_cols[0, 1, r : r + 1] = fields[0, r, cols - 1 : cols]
+    edges(0)
+    for copy in small[2:]:
+        copy.wait()
+    for s, lines in enumerate(code_columns()):
+        for r, line in enumerate(lines):
+            code_table[s, r] = line
     pl.semaphore_wait(barrier, peers - 1)
     send(0, (ABOVE, BELOW, LEFT, RIGHT))
-    step(0, True)
-
-    @pl.loop(1, basis - 1)
+    inside(0, True)
+    gather_rim()
+
+    @pl.loop(0, basis - 1)
     def _(k):
-        step(k, False)
-
-    step(basis - 1, False)
+        receive(k)
+        rim(k)
+        edges(k + 1)
+        send(k + 1, (ABOVE, BELOW, LEFT, RIGHT))
+        inside(k + 1, False)
+        inner(k)
+
+    receive(basis - 1)
+    rim(basis - 1)
+    inner(basis - 1)
 
     def deliver(d):
         return pltpu.make_async_remote_copy(
@@ -248,8 +286,9 @@
         column = jnp.broadcast_to(total[:, i : i + 1], (basis, tile))
         spread[i] = column
         proj.append(column)
+    turned = total.T
     for g in range(groups_prev):
-        proj_ref[g * basis : (g + 1) * basis, :] = total[:, g * basis : (g + 1) * basis]
+        proj_ref[:, g * basis : (g + 1) * basis] = turned[g * basis : (g + 1) * basis, :]
 
     cleaned = []
     for k in range(basis):
@@ -315,41 +354,49 @@
     basis, prev = shifts.shape[0], earlier.shape[0]
     peers = n_rows * n_cols
     vmem = pl.BlockSpec(memory_space=pltpu.VMEM)
-    smem = pl.BlockSpec(memory_space=pltpu.SMEM)
-    anywhere = pl.BlockSpec(memory_space=pl.ANY)
+    hbm = pl.BlockSpec(memory_space=pltpu.HBM)
+    codes = jnp.transpose(tile_codes, (2, 0, 1))
     f32 = jnp.float32
-    return pl.pallas_call(
+    basis_out, upper, proj = pl.pallas_call(
         functools.partial(kernel, n_rows, n_cols),
         out_shape=(
             jax.ShapeDtypeStruct((basis, rows, cols, tile), f32),
             jax.ShapeDtypeStruct((basis, basis), f32),
-            jax.ShapeDtypeStruct((prev, basis), f32),
+            jax.ShapeDtypeStruct((basis, prev), f32),
         ),
-        in_specs=[anywhere, vmem, smem, smem, anywhere, smem],
+        in_specs=[hbm] * 6,
         out_specs=(vmem, vmem, vmem),
         scratch_shapes=[
             pltpu.VMEM(tile_blocks.shape, f32),
             pltpu.VMEM(earlier.shape, f32),
+            pltpu.VMEM(codes.shape, jnp.int32),
+            pltpu.SMEM(shifts.shape, f32),
+            pltpu.SMEM(shift_order.shape, jnp.int32),
+            pltpu.SMEM(start_weights.shape, f32),
             pltpu.VMEM((basis + 1, rows, cols, tile), f32),
             pltpu.VMEM((slots, rows, cols, tile), f32),
             pltpu.VMEM((basis, 2, cols, tile), f32),
             pltpu.VMEM((basis, 2, rows, tile), f32),
             pltpu.VMEM((basis, 2, rows, tile), f32),
+            pltpu.VMEM((2, cols, tile, tile), f32),
+            pltpu.VMEM((2, rows, tile, tile), f32),
+            pltpu.VMEM((slots - 1, rows, cols, tile), f32),
             pltpu.VMEM((basis, tile), f32),
             pltpu.VMEM((peers, basis, tile), f32),
             pltpu.VMEM(((prev // basis + 1) * basis, basis, tile), f32),
             pltpu.SemaphoreType.DMA((rows, cols)),
-            pltpu.SemaphoreType.DMA,
+            pltpu.SemaphoreType.DMA((5,)),
             pltpu.SemaphoreType.DMA((basis, 4)),
             pltpu.SemaphoreType.DMA((basis, 4)),
             pltpu.SemaphoreType.DMA((peers,)),
             pltpu.SemaphoreType.DMA((peers,)),
         ],
         compiler_params=pltpu.CompilerParams(
-            collective_id=0, has_side_effects=True, vmem_limit_bytes=48 * 1024 * 1024
+            collective_id=0, has_side_effects=True, vmem_limit_bytes=67_043_328
         ),
         name="sstep",
-    )(tile_blocks, tile_codes, shifts, shift_order, earlier, start_weights)
+    )(tile_blocks, codes, shifts, shift_order, earlier, start_weights)
+    return basis_out, upper, proj.T
 
 
 def solution(mesh):

time: 44.9 us -> 42.6 us (0.949)
  local copies, waits for them, and re-layouts: 5.61 us -> 4.11 us
  Pallas kernels: 38.4 us -> 37.6 us
    pallas_call x1, Pallas kernels: 38.4 us -> 37.6 us  [shards(): pl.pallas_call(functools.partial(kernel, n_rows, n_cols), out_shape=(jax....]
    unnamed x11 -> x3, local copies, waits for them, and re-layouts: 4.94 us -> 4.11 us
    pallas_call x1 -> x0, local copies, waits for them, and re-layouts: 0.66 us -> none  [shards(): pl.pallas_call(functools.partial(kernel, n_rows, n_cols), out_shape=(jax....]
where the time goes in v1:
time: 42.6 us; the launch traced here: 42.3 us
  Pallas kernels  37.6 us (88%)
  local copies, waits for them, and re-layouts  4.11 us (10%)
  between operations  0.64 us (2%)
    pallas_call x1, Pallas kernels, shards(): pl.pallas_call(functools.partial(kernel, n_rows, n_cols), out_shape=(jax....  37.6 us
    unnamed x3, local copies, waits for them, and re-layouts  4.11 us

profile of v1, /device:TPU:0, one launch (start us, length us, event | category | flops | bytes accessed | tf_op | source)
XLA Modules:
  0.0 42.3 jit_solution(16061600237290615293)
XLA Ops:
  0.6 37.6 %sstep.1 = (f32[8,4,8,128]{3,2,1,0:T(8,128)}, f32[8,8]{1,0:T(8,128)}, f32[8,16]{1,0:T(8,128)}) custom-call(f32[4,8,4,128,128]{4,3,2,1,0:T(8,128)} %blocks_hbm.1, s32[3,4,8]{2,1,0:T(4,128)} %bitcast.2, f32[8]{0:T(128)} %shifts_hbm.1, s32[8]{0:T(128)} %order_hbm.1, f32[16,4,8,128]{3,2,1,0:T(8,128)} %earlier_hbm.1, f32[16]{0:T(128)} %weights_hbm.1), custom_call_target="tpu_custom_call" | custom-call | tf_op jit(solution)/shard_map/sstep/pallas_call | solution.py:360
  38.2 1.6 %copy.12 = f32[8,4,8,128]{3,2,1,0:T(8,128)} copy(f32[8,4,8,128]{3,2,1,0:T(8,128)} %get-tuple-element.12) | data formatting | bytes 262144
  39.8 1.3 %copy.13 = f32[8,8]{1,0:T(8,128)} copy(f32[8,8]{1,0:T(8,128)} %get-tuple-element.13) | data formatting | bytes 512
  41.1 1.3 %copy.14 = f32[16,8]{0,1:T(8,128)} copy(f32[16,8]{0,1:T(8,128)} %bitcast.3) | data formatting | bytes 1024
